TPU v7x, 32 devices: a whole 2x2x4 slice. The times are simulated.
32 devices in a mesh: row: 8 (over y, x, core), col: 4 (over z).
Axes of the slice: x: 2, y: 2, z: 4, core: 2. Of those that a mesh axis runs over, the one named last changes fastest.
Arguments:
- coeffs: bfloat16 [6144, 4096], P('row', 'col'), may hold values from -0.00390625 to 0.00390625
- occupation: float32 [4096], P('col'), may hold values from 0.5 to 2
- basis_on_grid: bfloat16 [320, 512, 512], P('row'), may hold values from -6 to 6
- basis_map: int32 [320, 512], P('row'), may hold values from 0 to 6143, as said below
- basis_count: int32 [320], P('row'), may hold values from 256 to 512
- batch_atom: int32 [320], P('row'), may hold values from 0 to 63
- harmonics: float32 [320, 49, 512], P('row'), may hold values from -0.25 to 0.25
Outputs:
- density: float32 [320, 512], P('row', 'col')
- moments: float32 [64, 49], replicated
Inputs may be any that keep to these rules, and one draw needn't show every extreme that they name: `basis_map`: the slots of one batch name distinct basis functions. With R = 768 and o = b // 40, batch b names only basis functions q * R + (o * 96 + w) mod R with 0 <= q < 8 and 0 <= w < 96.
All inputs are finite; a program needn't handle non-finite values.
Results may differ from a plain program's by a relative error of at most 0.0003.
Values may be sent and summed in bfloat16 or wider, within the bound.
A program may use at most 192 MiB of HBM per device.

v0:
```python
import jax
import jax.numpy as jnp
from jax import lax
from jax.sharding import PartitionSpec as P

WIN = 96
NATOM = 64


def shards(coeffs, occupation, basis_on_grid, basis_map, basis_count, batch_atom, harmonics):
    batches, points, slots = basis_on_grid.shape
    owned = coeffs.shape[0]
    owners = lax.axis_size("row")
    target = lax.broadcasted_iota(jnp.int32, (owners, WIN), 0)
    offset = lax.broadcasted_iota(jnp.int32, (owners, WIN), 1)
    outgoing_ids = jnp.mod(target * WIN + offset, owned).reshape(-1)
    outgoing = jnp.take(coeffs, outgoing_ids, axis=0)
    window = lax.all_to_all(outgoing, "row", split_axis=0, concat_axis=0, tiled=True)
    start = jnp.mod(lax.axis_index("row") * WIN, owned)
    source = basis_map // owned
    within = jnp.mod(basis_map % owned - start, owned)
    local_ids = source * WIN + within
    selected = jnp.take(window, local_ids, axis=0)
    slot_ids = lax.broadcasted_iota(jnp.int32, (batches, slots), 1)
    keep = slot_ids < basis_count[:, None]
    masked = jnp.where(keep[:, None, :], basis_on_grid, jnp.zeros_like(basis_on_grid))
    orbital = jnp.einsum("bps,bsk->bpk", masked, selected, preferred_element_type=jnp.float32)
    partial_density = jnp.sum(orbital * orbital * occupation[None, None, :], axis=2)
    atom_ids = lax.broadcasted_iota(jnp.int32, (batches, NATOM), 1)
    member = (batch_atom[:, None] == atom_ids).astype(jnp.float32)
    full_density = lax.psum(partial_density, "col")
    local_moment = jnp.einsum(
        "blp,bp->bl", harmonics, full_density, precision=lax.Precision.HIGHEST
    )
    atom_part = jnp.dot(member.T, local_moment, precision=lax.Precision.HIGHEST)
    moments = lax.psum(atom_part, "row")
    share = points // lax.axis_size("col")
    density = lax.dynamic_slice_in_dim(full_density, lax.axis_index("col") * share, share, 1)
    return (density, moments)


def solution(mesh):
    placed = (
        P("row", "col"),
        P("col"),
        P("row", None, None),
        P("row", None),
        P("row"),
        P("row"),
        P("row", None, None),
    )
    return jax.shard_map(
        shards, mesh=mesh, in_specs=placed, out_specs=(P("row", "col"), P()), check_vma=False
    )
```

profile of v0, /device:TPU:0, one launch (start us, length us, event | category | flops | bytes accessed | tf_op | source)
XLA Modules:
  0.0 228.4 jit_solution(9429908495071229577)
XLA Ops:
  7.2 0.0 copy-start
  7.2 0.1 add_remainder_fusion
  7.3 0.1 compare_and_fusion.1
  7.4 0.1 rem.52
  7.5 1.1 copy-done
  8.6 2.8 %gather_fusion = bf16[768,1024]{1,0:T(8,128)(2,1)S(1)} fusion(bf16[768,1024]{1,0:T(8,128)(2,1)S(1)} %copy-done, s32[1024]{0:T(1024)S(1)} %pad_clamp_fusion), kind=kCustom, calls=%fused_computation | custom fusion | bytes 3148800 | tf_op jit(solution)/shard_map/jit(_take)/gather | solution.py:17
  11.4 1.4 broadcast_select_fusion
  12.8 5.2 %all-to-all-start = ((bf16[8,96,1024]{2,1,0:T(8,128)(2,1)}), bf16[8,96,1024]{2,1,0:T(8,128)(2,1)S(1)}, u32[]{:S(2)}, u32[]{:S(2)}) async-start(bf16[8,96,1024]{2,1,0:T(8,128)(2,1)} %broadcast_select_fusion), calls=%async_computation | async-start | bytes 3145728 | tf_op jit(solution)/shard_map/all_to_all | solution.py:18
  18.0 0.0 all-reduce.2.cloned.1.call-start
  18.0 1.0 compare_and_fusion
  19.1 0.7 iota_compare_fusion
  19.9 19.1 %all-to-all-done = bf16[8,96,1024]{2,1,0:T(8,128)(2,1)S(1)} async-done(((bf16[8,96,1024]{2,1,0:T(8,128)(2,1)}), bf16[8,96,1024]{2,1,0:T(8,128)(2,1)S(1)}, u32[]{:S(2)}, u32[]{:S(2)}) %all-to-all-start) | async-done | bytes 1572896 | tf_op jit(solution)/shard_map/all_to_all | solution.py:18
  39.0 0.0 copy-start.2
  39.0 87.0 %gather_fusion.1 = bf16[20480,1024]{1,0:T(8,128)(2,1)} fusion(bf16[768,1024]{1,0:T(8,128)(2,1)S(1)} %bitcast.9, s32[20480]{0:T(1024)S(1)} %broadcast_clamp_fusion), kind=kCustom, calls=%fused_computation.1 | custom fusion | bytes 83968000 | tf_op jit(solution)/shard_map/jit(_take)/gather | solution.py:23
  125.9 0.0 copy-done.2
  125.9 0.0 copy-start.3
  125.9 0.0 copy-start.1
  125.9 29.3 %multiply_reduce_fusion = f32[40,512]{1,0:T(8,128)} fusion(f32[1024]{0:T(1024)S(1)} %copy-done.2, bf16[40,512,1024]{2,1,0:T(8,128)(2,1)} %bitcast.10, pred[40,512]{1,0:T(8,128)(4,1)S(1)} %get-tuple-element.2, bf16[40,512,512]{2,1,0:T(8,128)(2,1)} %param.9, pred[40,512]{1,0:T(8,128)(4,1)S(1)} %iota_compare_fusion), kind=kOutput, calls=%fused_computation.2 | convolution fusion | flops 21569187840 | bytes 63041536 | tf_op jit(solution)/shard_map/bps,bsk->bpk/dot_general | solution.py:27
  155.2 0.0 all-reduce.2.cloned.1.call-update
  155.3 33.8 %all-reduce.2.cloned.1.call-done = f32[40,512]{1,0:T(8,128)} async-done(((f32[40,512]{1,0:T(8,128)}), f32[40,512]{1,0:T(8,128)}) %all-reduce.2.cloned.1.call-update) | async-done | bytes 81936 | tf_op jit(solution)/shard_map/psum | solution.py:31
  189.0 7.9 %fusion.11 = f32[40,1,49]{2,1,0:T(1,128)S(1)} fusion(f32[40,49,512]{2,0,1:T(8,128)} %param.13, f32[40,512,1]{1,0,2:T(8,128)} %bitcast.14), kind=kOutput, calls=%fused_computation.10 | convolution fusion | flops 12042240 | bytes 4103840 | tf_op jit(solution)/shard_map/blp,bp->bl/dot_general | solution.py:32
  196.9 0.0 copy-done.3
  196.9 0.2 fusion.19
  197.2 23.0 %psum.15 = f32[64,49]{0,1:T(8,128)} all-reduce(f32[64,49]{0,1:T(8,128)S(1)} %fusion.19), channel_id=1, replica_groups=mesh['row'=8,'col'=4] {'row'}, use_global_device_ids=true, to_apply=%region_2.3 | all-reduce | flops 3136 | bytes 25088 | tf_op jit(solution)/shard_map/psum | solution.py:36
  220.2 1.3 constant_dynamic-slice_fusion
  221.5 0.0 copy-done.1
  (5 shorter events, 0.1 us)
Async XLA Ops:
  7.2 1.4 copy-start
  12.8 26.2 %all-to-all-start = ((bf16[8,96,1024]{2,1,0:T(8,128)(2,1)}), bf16[8,96,1024]{2,1,0:T(8,128)(2,1)S(1)}, u32[]{:S(2)}, u32[]{:S(2)}) async-start(bf16[8,96,1024]{2,1,0:T(8,128)(2,1)} %broadcast_select_fusion), calls=%async_computation | async-start | bytes 3145728 | tf_op jit(solution)/shard_map/all_to_all | solution.py:18
  18.0 171.1 %all-reduce.2.cloned.1.call-start = ((), (), s32[]{:S(2)}) async-start(), calls=%async_computation.1 | async-start | bytes 163840 | tf_op jit(solution)/shard_map/psum | solution.py:31
  39.0 87.0 %copy-start.2 = (f32[1024]{0:T(1024)S(1)}, f32[1024]{0:T(1024)}, u32[]{:S(2)}) copy-start(f32[1024]{0:T(1024)} %param.8) | copy-start | bytes 12292
  125.9 71.0 %copy-start.3 = (s32[40]{0:T(128)S(1)}, s32[40]{0:T(128)}, u32[]{:S(2)}) copy-start(s32[40]{0:T(128)} %param.12) | copy-start | bytes 484
  125.9 95.6 %copy-start.1 = (bf16[768,1024]{1,0:T(8,128)(2,1)S(1)}, bf16[768,1024]{1,0:T(8,128)(2,1)}, u32[]{:S(2)}) copy-start(bf16[768,1024]{1,0:T(8,128)(2,1)} %param.7) | copy-start | bytes 4718596
Sparse Core Ops, SparseCore 0:
  155.4 33.6 all-reduce.1
where the time goes:
time: 229 us; the launch traced here: 228 us
  local copies, waits for them, and re-layouts  92.3 us (40%)
  waiting for transfers between devices  52.9 us (23%)
  matrix products  37.5 us (16%)
  blocking collectives  23 us (10%)
  between operations  14.1 us (6%)
  starting transfers between devices  5.24 us (2%)
  other arithmetic  3.37 us (1%)
    gather x1, local copies, waits for them, and re-layouts, shards(): selected = jnp.take(window, local_ids, axis=0)  87 us
    psum x1, waiting for transfers between devices, shards(): full_density = lax.psum(partial_density, 'col')  33.8 us
    dot_general x1, matrix products, shards(): jnp.einsum('bps,bsk->bpk', masked, selected, preferred_element_type=jnp.f...  29.3 us
    psum x1, blocking collectives, shards(): moments = lax.psum(atom_part, 'row')  23 us
    all_to_all x1, waiting for transfers between devices, shards(): lax.all_to_all(outgoing, 'row', split_axis=0, concat_axis=0, tiled=True)  19.1 us
    dot_general x1, matrix products, shards(): jnp.einsum('blp,bp->bl', harmonics, full_density, precision=lax.Precision...  7.89 us
    all_to_all x1, starting transfers between devices, shards(): lax.all_to_all(outgoing, 'row', split_axis=0, concat_axis=0, tiled=True)  5.2 us
  transfers between devices with their start and end apart: 2, of which 2 were waited for; matrix products, arithmetic and copies ran while one was open for 1% of the time, Pallas kernels for 0%

commit v1 on v0

--- a/solution.py
+++ b/solution.py
@@ -1,13 +1,19 @@
+import functools
+
 import jax
 import jax.numpy as jnp
 from jax import lax
+from jax.experimental import pallas as pl
+from jax.experimental.pallas import tpu as pltpu
 from jax.sharding import PartitionSpec as P
 
 WIN = 96
 NATOM = 64
-
-
-def shards(coeffs, occupation, basis_on_grid, basis_map, basis_count, batch_atom, harmonics):
+VMEM_BYTES = 62 * 1024 * 1024
+DEPTH = 3
+
+
+def plain(coeffs, occupation, basis_on_grid, basis_map, basis_count, batch_atom, harmonics):
     batches, points, slots = basis_on_grid.shape
     owned = coeffs.shape[0]
     owners = lax.axis_size("row")
@@ -26,16 +32,164 @@
     masked = jnp.where(keep[:, None, :], basis_on_grid, jnp.zeros_like(basis_on_grid))
     orbital = jnp.einsum("bps,bsk->bpk", masked, selected, preferred_element_type=jnp.float32)
     partial_density = jnp.sum(orbital * orbital * occupation[None, None, :], axis=2)
+    full_density = lax.psum(partial_density, "col")
+    share = points // lax.axis_size("col")
+    return lax.dynamic_slice_in_dim(full_density, lax.axis_index("col") * share, share, 1)
+
+
+def kernel(rows, cols, owned, coeffs, occ, basis, index, count, out,
+           held, window, across, weight, spread, dens, got,
+           own_sem, in_sem, send_sem, recv_sem, dsend_sem, drecv_sem):
+    batches, points, slots = basis.shape
+    states = coeffs.shape[1]
+    me, mine = lax.axis_index("row"), lax.axis_index("col")
+    share = points // cols
+
+    barrier = pltpu.get_barrier_semaphore()
+    for k in range(1, rows):
+        pl.semaphore_signal(barrier, inc=1, device_id={"row": lax.rem(me + k, rows)},
+                            device_id_type=pl.DeviceIdType.MESH)
+    for k in range(1, cols):
+        pl.semaphore_signal(barrier, inc=1, device_id={"col": lax.rem(mine + k, cols)},
+                            device_id_type=pl.DeviceIdType.MESH)
+
+    def fetch(b, slot):
+        return pltpu.make_async_copy(basis.at[b], held.at[slot], in_sem.at[slot])
+
+    for b in range(DEPTH - 1):
+        fetch(b, b).start()
+    here = pl.ds(pl.multiple_of(me * WIN, 32), WIN)
+
+    def rows_for(owner):
+        return coeffs.at[pl.ds(pl.multiple_of(lax.rem(owner * WIN, owned), 32), WIN), :]
+
+    own = pltpu.make_async_copy(rows_for(me), window.at[here, :], own_sem)
+    own.start()
+    pl.semaphore_wait(barrier, rows + cols - 2)
+    sends = []
+    for k in range(1, rows):
+        peer = lax.rem(me + k, rows)
+        copy = pltpu.make_async_remote_copy(
+            src_ref=rows_for(peer), dst_ref=window.at[here, :],
+            send_sem=send_sem.at[k - 1], recv_sem=recv_sem.at[k - 1],
+            device_id={"row": peer}, device_id_type=pl.DeviceIdType.MESH)
+        copy.start()
+        sends.append(copy)
+
+    for j in range(states // 128):
+        line = jnp.broadcast_to(occ[j:j + 1, :], (128, 128))
+        weight[j * 128:(j + 1) * 128, :] = line.T
+
+    start = lax.rem(me * WIN, owned)
+    row_of = lax.broadcasted_iota(jnp.int32, (WIN, 1), 0) + start
+    name = jnp.concatenate([row_of + r * owned for r in range(rows)], axis=0)
+    lane = lax.broadcasted_iota(jnp.int32, (1, slots), 1)
+
+    def scatter(b, carry):
+        slot = lax.rem(b, DEPTH)
+        ahead = b + DEPTH - 1
+
+        @pl.when(ahead < batches)
+        def _():
+            fetch(ahead, lax.rem(ahead, DEPTH)).start()
+
+        fetch(b, slot).wait()
+        ids = jnp.where(lane < count[b], index[pl.ds(b, 1), :], -1)
+        hot = jnp.where(name == ids, 1.0, 0.0).astype(jnp.bfloat16)
+        moved = lax.dot_general(hot, held[slot], (((1,), (1,)), ((), ())),
+                                preferred_element_type=jnp.float32)
+        spread[b] = moved.astype(jnp.bfloat16)
+        return carry
+
+    lax.fori_loop(0, batches, scatter, 0)
+
+    own.wait()
+    for copy in sends:
+        copy.wait()
+    for j in range(states // 128):
+        across[j * 128:(j + 1) * 128, :] = window[:, j * 128:(j + 1) * 128].T
+
+    def square(b, carry):
+        values = spread[b]
+        total = jnp.zeros((8, points), jnp.float32)
+        step = 256
+        for n in range(0, states, step):
+            orbital = lax.dot_general(across[n:n + step, :], values, (((1,), (0,)), ((), ())),
+                                      preferred_element_type=jnp.float32)
+            scale = weight[n:n + step, :]
+            scale = jnp.concatenate([scale] * (points // 128), axis=1)
+            term = orbital * orbital * scale
+            total = total + jnp.sum(term.reshape(step // 8, 8, points), axis=0)
+        line = jnp.sum(total, axis=0, keepdims=True)
+        for c in range(cols):
+            dens[c, pl.ds(b, 1), :] = line[:, c * share:(c + 1) * share]
+        return carry
+
+    lax.fori_loop(0, batches, square, 0)
+
+    copies = []
+    for k in range(1, cols):
+        peer = lax.rem(mine + k, cols)
+        copy = pltpu.make_async_remote_copy(
+            src_ref=dens.at[peer], dst_ref=got.at[k - 1],
+            send_sem=dsend_sem.at[k - 1], recv_sem=drecv_sem.at[k - 1],
+            device_id={"col": peer}, device_id_type=pl.DeviceIdType.MESH)
+        copy.start()
+        copies.append(copy)
+    result = dens[mine]
+    for k, copy in enumerate(copies):
+        copy.wait()
+        result = result + got[k]
+    out[...] = result
+
+
+def density_of(coeffs, occupation, basis_on_grid, basis_map, basis_count):
+    batches, points, slots = basis_on_grid.shape
+    owned, states = coeffs.shape
+    rows, cols = lax.axis_size("row"), lax.axis_size("col")
+    reach = rows * WIN
+    vmem, dma = pltpu.VMEM, pltpu.SemaphoreType.DMA
+    half, single = jnp.bfloat16, jnp.float32
+    whole = pl.BlockSpec(memory_space=pltpu.VMEM)
+    apart = pl.BlockSpec(memory_space=pl.ANY)
+    return pl.pallas_call(
+        functools.partial(kernel, rows, cols, owned),
+        out_shape=jax.ShapeDtypeStruct((batches, points // cols), single),
+        in_specs=[apart, whole, apart, whole, pl.BlockSpec(memory_space=pltpu.SMEM)],
+        out_specs=whole,
+        scratch_shapes=[
+            vmem((DEPTH, points, slots), half),
+            vmem((reach, states), half),
+            vmem((states, reach), half),
+            vmem((states, 128), single),
+            vmem((batches, reach, points), half),
+            vmem((cols, batches, points // cols), single),
+            vmem((cols - 1, batches, points // cols), single),
+            dma, dma((DEPTH,)), dma((rows - 1,)), dma((rows - 1,)),
+            dma((cols - 1,)), dma((cols - 1,)),
+        ],
+        compiler_params=pltpu.CompilerParams(
+            collective_id=0, has_side_effects=True, vmem_limit_bytes=VMEM_BYTES),
+    )(coeffs, occupation.reshape(-1, 128), basis_on_grid, basis_map, basis_count)
+
+
+def shards(coeffs, occupation, basis_on_grid, basis_map, basis_count, batch_atom, harmonics):
+    batches, points, slots = basis_on_grid.shape
+    owned, states = coeffs.shape
+    cols, reach = lax.axis_size("col"), lax.axis_size("row") * WIN
+    share = points // cols
+    needed = batches * reach * points * 2 + 4 * reach * states
+    if needed < VMEM_BYTES * 3 // 4 and share % 128 == 0 and owned % WIN == 0:
+        density = density_of(coeffs, occupation, basis_on_grid, basis_map, basis_count)
+    else:
+        density = plain(coeffs, occupation, basis_on_grid, basis_map, basis_count,
+                        batch_atom, harmonics)
+    part = lax.dynamic_slice_in_dim(harmonics, lax.axis_index("col") * share, share, 2)
+    local_moment = jnp.sum(part * density[:, None, :], axis=2)
     atom_ids = lax.broadcasted_iota(jnp.int32, (batches, NATOM), 1)
     member = (batch_atom[:, None] == atom_ids).astype(jnp.float32)
-    full_density = lax.psum(partial_density, "col")
-    local_moment = jnp.einsum(
-        "blp,bp->bl", harmonics, full_density, precision=lax.Precision.HIGHEST
-    )
     atom_part = jnp.dot(member.T, local_moment, precision=lax.Precision.HIGHEST)
-    moments = lax.psum(atom_part, "row")
-    share = points // lax.axis_size("col")
-    density = lax.dynamic_slice_in_dim(full_density, lax.axis_index("col") * share, share, 1)
+    moments = lax.psum(atom_part, ("row", "col"))
     return (density, moments)
 
 

time: 229 us -> 120 us (0.52)
  local copies, waits for them, and re-layouts: 92.3 us -> 1.34 us
  Pallas kernels: 0 us -> 76.6 us
  waiting for transfers between devices: 52.9 us -> 0 us
  matrix products: 37.5 us -> 0.22 us
  blocking collectives: 23 us -> 39.3 us
  between operations: 14.1 us -> 0.67 us
  starting transfers between devices: 5.24 us -> 0 us
    gather x2 -> x0, local copies, waits for them, and re-layouts: 89.8 us -> none  [the longest x1 87 us: shards(): selected = jnp.take(window, local_ids, axis=0)]
    pallas_call x0 -> x1, Pallas kernels: none -> 76.6 us  [density_of(): pl.pallas_call(functools.partial(kernel, rows, cols, owned), out_shape=ja...]
    dot_general x2 -> x0, matrix products: 37.2 us -> none  [the longest x1 29.3 us: shards(): jnp.einsum('bps,bsk->bpk', masked, selected, preferred_element_type=jnp.f...]
    psum x1 -> x0, waiting for transfers between devices: 33.8 us -> none  [shards(): full_density = lax.psum(partial_density, 'col')]
    all_to_all x1 -> x0, waiting for transfers between devices: 19.1 us -> none  [shards(): lax.all_to_all(outgoing, 'row', split_axis=0, concat_axis=0, tiled=True)]
    psum x1, blocking collectives: 23 us -> 39.3 us  [shards(): moments = lax.psum(atom_part, ('row', 'col'))]
    all_to_all x1 -> x0, starting transfers between devices: 5.2 us -> none  [shards(): lax.all_to_all(outgoing, 'row', split_axis=0, concat_axis=0, tiled=True)]
  transfers between devices with their start and end apart: 2 -> 0, of which waited for: 2 -> 0; matrix products, arithmetic and copies ran while one was open for 1% -> 0% of each run, Pallas kernels for 0% -> 0%
where the time goes in v1:
time: 120 us
  Pallas kernels  76.6 us (64%)
  blocking collectives  39.3 us (33%)
  other arithmetic  1.55 us (1%)
  local copies, waits for them, and re-layouts  1.34 us (1%)
    pallas_call x1, Pallas kernels, density_of(): pl.pallas_call(functools.partial(kernel, rows, cols, owned), out_shape=ja...  76.6 us
    psum x1, blocking collectives, shards(): moments = lax.psum(atom_part, ('row', 'col'))  39.3 us

profile of v1, /device:TPU:0, one launch (start us, length us, event | category | flops | bytes accessed | tf_op | source)
XLA Modules:
  0.0 119.6 jit_solution(10347177329007320199)
XLA Ops:
  0.6 0.0 copy-start
  0.6 76.6 %shard_map.86 = f32[40,128]{1,0:T(8,128)} custom-call(bf16[768,1024]{1,0:T(8,128)(2,1)} %coeffs.1, f32[8,128]{1,0:T(8,128)} %bitcast.2, bf16[40,512,512]{2,1,0:T(8,128)(2,1)} %basis.1, s32[40,512]{1,0:T(8,128)} %index.1, s32[40]{0:T(128)} %count.1), custom_call_target="tpu_custom_call" | custom-call | tf_op jit(solution)/shard_map/pallas_call | solution.py:155
  77.2 1.6 %multiply_reduce_fusion = f32[40,49]{0,1:T(8,128)S(1)} fusion(f32[40,49,512]{2,0,1:T(8,128)} %param.13, s32[]{:T(128)S(6)} %select_n.3, f32[40,128]{1,0:T(8,128)} %shard_map.86), kind=kLoop, calls=%fused_computation | loop fusion | flops 499800 | bytes 1031844 | tf_op jit(solution)/shard_map/reduce_sum | solution.py:188
  78.8 0.0 copy-done
  78.8 0.2 fusion
  79.0 39.3 %psum.7 = f32[64,49]{0,1:T(8,128)} all-reduce(f32[64,49]{0,1:T(8,128)S(1)} %fusion), channel_id=1, replica_groups=mesh['row'=8,'col'=4] {'row','col'}, use_global_device_ids=true, to_apply=%region_1.0 | all-reduce | flops 3136 | bytes 25088 | tf_op jit(solution)/shard_map/psum | solution.py:192
  118.3 1.3 %copy.10 = f32[40,128]{1,0:T(8,128)} copy(f32[40,128]{1,0:T(8,128)} %shard_map.86) | data formatting | bytes 40960
Async XLA Ops:
  0.6 78.1 %copy-start = (s32[40]{0:T(128)S(1)}, s32[40]{0:T(128)}, u32[]{:S(2)}) copy-start(s32[40]{0:T(128)} %param.12) | copy-start | bytes 484

commit v2 on v1

--- a/solution.py
+++ b/solution.py
@@ -13,7 +13,7 @@
 DEPTH = 3
 
 
-def plain(coeffs, occupation, basis_on_grid, basis_map, basis_count, batch_atom, harmonics):
+def plain(coeffs, occupation, basis_on_grid, basis_map, basis_count):
     batches, points, slots = basis_on_grid.shape
     owned = coeffs.shape[0]
     owners = lax.axis_size("row")
@@ -37,9 +37,10 @@
     return lax.dynamic_slice_in_dim(full_density, lax.axis_index("col") * share, share, 1)
 
 
-def kernel(rows, cols, owned, coeffs, occ, basis, index, count, out,
-           held, window, across, weight, spread, dens, got,
-           own_sem, in_sem, send_sem, recv_sem, dsend_sem, drecv_sem):
+def kernel(rows, cols, owned, coeffs, occ, basis, index, count, atom, harmonics, out, out_moments,
+           held, window, across, weight, spread, angular, dens, got, near, far, moment,
+           own_sem, in_sem, angular_sem, send_sem, recv_sem, dsend_sem, drecv_sem,
+           nsend_sem, nrecv_sem, fsend_sem, frecv_sem):
     batches, points, slots = basis.shape
     states = coeffs.shape[1]
     me, mine = lax.axis_index("row"), lax.axis_index("col")
@@ -65,6 +66,8 @@
 
     own = pltpu.make_async_copy(rows_for(me), window.at[here, :], own_sem)
     own.start()
+    load = pltpu.make_async_copy(harmonics, angular, angular_sem)
+    load.start()
     pl.semaphore_wait(barrier, rows + cols - 2)
     sends = []
     for k in range(1, rows):
@@ -108,6 +111,10 @@
         copy.wait()
     for j in range(states // 128):
         across[j * 128:(j + 1) * 128, :] = window[:, j * 128:(j + 1) * 128].T
+
+    load.wait()
+    moment[...] = jnp.zeros_like(moment)
+    atoms = lax.broadcasted_iota(jnp.int32, (1, 128), 1)
 
     def square(b, carry):
         values = spread[b]
@@ -123,27 +130,54 @@
         line = jnp.sum(total, axis=0, keepdims=True)
         for c in range(cols):
             dens[c, pl.ds(b, 1), :] = line[:, c * share:(c + 1) * share]
+        local = jnp.sum(angular[b] * line, axis=1, keepdims=True)
+        moment[...] += local * jnp.where(atoms == atom[b], 1.0, 0.0)
         return carry
 
     lax.fori_loop(0, batches, square, 0)
 
-    copies = []
-    for k in range(1, cols):
-        peer = lax.rem(mine + k, cols)
-        copy = pltpu.make_async_remote_copy(
-            src_ref=dens.at[peer], dst_ref=got.at[k - 1],
-            send_sem=dsend_sem.at[k - 1], recv_sem=drecv_sem.at[k - 1],
-            device_id={"col": peer}, device_id_type=pl.DeviceIdType.MESH)
-        copy.start()
-        copies.append(copy)
+    def exchange(axis, place, size, src_of, dst_of, sent, received):
+        copies = []
+        for k in range(1, size):
+            peer = lax.rem(place + k, size)
+            copy = pltpu.make_async_remote_copy(
+                src_ref=src_of(peer), dst_ref=dst_of(k),
+                send_sem=sent.at[k - 1], recv_sem=received.at[k - 1],
+                device_id={axis: peer}, device_id_type=pl.DeviceIdType.MESH)
+            copy.start()
+            copies.append(copy)
+        return copies
+
+    moved = exchange("col", mine, cols, lambda peer: moment, lambda k: near.at[mine],
+                     nsend_sem, nrecv_sem)
+    copies = exchange("col", mine, cols, lambda peer: dens.at[peer], lambda k: got.at[k - 1],
+                      dsend_sem, drecv_sem)
+    near[mine] = moment[...]
+    for copy in moved:
+        copy.wait()
+    total = near[0]
+    for c in range(1, cols):
+        total = total + near[c]
+    moment[...] = total
+    far[me] = total
+    moved = exchange("row", me, rows, lambda peer: moment, lambda k: far.at[me],
+                     fsend_sem, frecv_sem)
     result = dens[mine]
     for k, copy in enumerate(copies):
         copy.wait()
         result = result + got[k]
     out[...] = result
-
-
-def density_of(coeffs, occupation, basis_on_grid, basis_map, basis_count):
+    for copy in moved:
+        copy.wait()
+    total = far[0]
+    for r in range(1, rows):
+        total = total + far[r]
+    count_l = total.shape[0]
+    total = jnp.concatenate([total, jnp.zeros((128 - count_l, 128), jnp.float32)], axis=0)
+    out_moments[...] = total.T[:NATOM, :count_l]
+
+
+def fused(coeffs, occupation, basis_on_grid, basis_map, basis_count, batch_atom, harmonics):
     batches, points, slots = basis_on_grid.shape
     owned, states = coeffs.shape
     rows, cols = lax.axis_size("row"), lax.axis_size("col")
@@ -151,26 +185,35 @@
     vmem, dma = pltpu.VMEM, pltpu.SemaphoreType.DMA
     half, single = jnp.bfloat16, jnp.float32
     whole = pl.BlockSpec(memory_space=pltpu.VMEM)
+    scalar = pl.BlockSpec(memory_space=pltpu.SMEM)
+    lm = harmonics.shape[1]
     apart = pl.BlockSpec(memory_space=pl.ANY)
     return pl.pallas_call(
         functools.partial(kernel, rows, cols, owned),
-        out_shape=jax.ShapeDtypeStruct((batches, points // cols), single),
-        in_specs=[apart, whole, apart, whole, pl.BlockSpec(memory_space=pltpu.SMEM)],
-        out_specs=whole,
+        out_shape=(jax.ShapeDtypeStruct((batches, points // cols), single),
+                   jax.ShapeDtypeStruct((NATOM, lm), single)),
+        in_specs=[apart, whole, apart, whole, scalar, scalar, apart],
+        out_specs=(whole, whole),
         scratch_shapes=[
             vmem((DEPTH, points, slots), half),
             vmem((reach, states), half),
             vmem((states, reach), half),
             vmem((states, 128), single),
             vmem((batches, reach, points), half),
+            vmem((batches, lm, points), single),
             vmem((cols, batches, points // cols), single),
             vmem((cols - 1, batches, points // cols), single),
-            dma, dma((DEPTH,)), dma((rows - 1,)), dma((rows - 1,)),
-            dma((cols - 1,)), dma((cols - 1,)),
+            vmem((cols, lm, 128), single),
+            vmem((rows, lm, 128), single),
+            vmem((lm, 128), single),
+            dma, dma((DEPTH,)), dma, dma((rows - 1,)), dma((rows - 1,)),
+            dma((cols - 1,)), dma((cols - 1,)), dma((cols - 1,)), dma((cols - 1,)),
+            dma((rows - 1,)), dma((rows - 1,)),
         ],
         compiler_params=pltpu.CompilerParams(
             collective_id=0, has_side_effects=True, vmem_limit_bytes=VMEM_BYTES),
-    )(coeffs, occupation.reshape(-1, 128), basis_on_grid, basis_map, basis_count)
+    )(coeffs, occupation.reshape(-1, 128), basis_on_grid, basis_map, basis_count,
+      batch_atom, harmonics)
 
 
 def shards(coeffs, occupation, basis_on_grid, basis_map, basis_count, batch_atom, harmonics):
@@ -180,10 +223,9 @@
     share = points // cols
     needed = batches * reach * points * 2 + 4 * reach * states
     if needed < VMEM_BYTES * 3 // 4 and share % 128 == 0 and owned % WIN == 0:
-        density = density_of(coeffs, occupation, basis_on_grid, basis_map, basis_count)
-    else:
-        density = plain(coeffs, occupation, basis_on_grid, basis_map, basis_count,
-                        batch_atom, harmonics)
+        return fused(coeffs, occupation, basis_on_grid, basis_map, basis_count,
+                     batch_atom, harmonics)
+    density = plain(coeffs, occupation, basis_on_grid, basis_map, basis_count)
     part = lax.dynamic_slice_in_dim(harmonics, lax.axis_index("col") * share, share, 2)
     local_moment = jnp.sum(part * density[:, None, :], axis=2)
     atom_ids = lax.broadcasted_iota(jnp.int32, (batches, NATOM), 1)

time: 120 us -> 94.2 us (0.79)
  blocking collectives: 39.3 us -> 0 us
  local copies, waits for them, and re-layouts: 1.34 us -> 9.35 us
  Pallas kernels: 76.6 us -> 83.9 us
  other arithmetic: 1.55 us -> 0 us
    psum x1 -> x0, blocking collectives: 39.3 us -> none  [shards(): moments = lax.psum(atom_part, ('row', 'col'))]
    pallas_call x1, Pallas kernels: 76.6 us -> 83.9 us  [fused(): pl.pallas_call(functools.partial(kernel, rows, cols, owned), out_shape=(j...]
    unnamed x3 -> x2, local copies, waits for them, and re-layouts: 1.34 us -> 7.9 us
    reduce_sum x1 -> x0, other arithmetic: 1.55 us -> none  [shards(): local_moment = jnp.sum(part * density[:, None, :], axis=2)]
    pallas_call x0 -> x1, local copies, waits for them, and re-layouts: none -> 1.45 us  [fused(): pl.pallas_call(functools.partial(kernel, rows, cols, owned), out_shape=(j...]
where the time goes in v2:
time: 94.2 us; the launch traced here: 93.9 us
  Pallas kernels  83.9 us (89%)
  local copies, waits for them, and re-layouts  9.35 us (10%)
    pallas_call x1, Pallas kernels, fused(): pl.pallas_call(functools.partial(kernel, rows, cols, owned), out_shape=(j...  83.9 us
    unnamed x2, local copies, waits for them, and re-layouts  7.9 us

profile of v2, /device:TPU:0, one launch (start us, length us, event | category | flops | bytes accessed | tf_op | source)
XLA Modules:
  0.0 93.9 jit_solution(18042065074444109947)
XLA Ops:
  0.6 6.6 %copy.9.harmonics = f32[40,49,512]{2,1,0:T(8,128)} copy(f32[40,49,512]{2,0,1:T(8,128)} %param.13) | data formatting | bytes 8028160 | tf_op args[6]
  7.2 83.9 %shard_map.86 = (f32[40,128]{1,0:T(8,128)}, f32[64,49]{1,0:T(8,128)}) custom-call(bf16[768,1024]{1,0:T(8,128)(2,1)} %coeffs.1, f32[8,128]{1,0:T(8,128)} %bitcast.1, bf16[40,512,512]{2,1,0:T(8,128)(2,1)} %basis.1, s32[40,512]{1,0:T(8,128)} %index.1, s32[40]{0:T(128)} %count.1, s32[40]{0:T(128)} %atom.1, f32[40,49,512]{2,1,0:T(8,128)} %copy.9.harmonics), custom_call_target="tpu_custom_call" | custom-call | tf_op jit(solution)/shard_map/pallas_call | solution.py:191
  91.1 1.5 %copy.10 = f32[64,49]{0,1:T(8,128)} copy(f32[64,49]{1,0:T(8,128)} %get-tuple-element.3) | data formatting | bytes 25088 | tf_op jit(solution)/shard_map/pallas_call | solution.py:191
  92.6 1.3 %copy.12 = f32[40,128]{1,0:T(8,128)} copy(f32[40,128]{1,0:T(8,128)} %get-tuple-element.6) | data formatting | bytes 40960

commit v3 on v2

--- a/solution.py
+++ b/solution.py
@@ -10,6 +10,7 @@
 WIN = 96
 NATOM = 64
 VMEM_BYTES = 62 * 1024 * 1024
+HALVES = 2
 DEPTH = 3
 
 
@@ -61,23 +62,26 @@
         fetch(b, b).start()
     here = pl.ds(pl.multiple_of(me * WIN, 32), WIN)
 
-    def rows_for(owner):
-        return coeffs.at[pl.ds(pl.multiple_of(lax.rem(owner * WIN, owned), 32), WIN), :]
+    def rows_for(owner, columns=slice(None)):
+        return coeffs.at[pl.ds(pl.multiple_of(lax.rem(owner * WIN, owned), 32), WIN), columns]
 
     own = pltpu.make_async_copy(rows_for(me), window.at[here, :], own_sem)
     own.start()
     load = pltpu.make_async_copy(harmonics, angular, angular_sem)
     load.start()
     pl.semaphore_wait(barrier, rows + cols - 2)
-    sends = []
-    for k in range(1, rows):
-        peer = lax.rem(me + k, rows)
-        copy = pltpu.make_async_remote_copy(
-            src_ref=rows_for(peer), dst_ref=window.at[here, :],
-            send_sem=send_sem.at[k - 1], recv_sem=recv_sem.at[k - 1],
-            device_id={"row": peer}, device_id_type=pl.DeviceIdType.MESH)
-        copy.start()
-        sends.append(copy)
+    width = states // HALVES
+    sends = [[] for _ in range(HALVES)]
+    for h in range(HALVES):
+        columns = pl.ds(h * width, width)
+        for k in range(1, rows):
+            peer = lax.rem(me + k, rows)
+            copy = pltpu.make_async_remote_copy(
+                src_ref=rows_for(peer, columns), dst_ref=window.at[here, columns],
+                send_sem=send_sem.at[h, k - 1], recv_sem=recv_sem.at[h, k - 1],
+                device_id={"row": peer}, device_id_type=pl.DeviceIdType.MESH)
+            copy.start()
+            sends[h].append(copy)
 
     for j in range(states // 128):
         line = jnp.broadcast_to(occ[j:j + 1, :], (128, 128))
@@ -107,20 +111,15 @@
     lax.fori_loop(0, batches, scatter, 0)
 
     own.wait()
-    for copy in sends:
-        copy.wait()
-    for j in range(states // 128):
-        across[j * 128:(j + 1) * 128, :] = window[:, j * 128:(j + 1) * 128].T
-
     load.wait()
     moment[...] = jnp.zeros_like(moment)
     atoms = lax.broadcasted_iota(jnp.int32, (1, 128), 1)
 
-    def square(b, carry):
+    def square(h, b, carry):
         values = spread[b]
         total = jnp.zeros((8, points), jnp.float32)
         step = 256
-        for n in range(0, states, step):
+        for n in range(h * width, (h + 1) * width, step):
             orbital = lax.dot_general(across[n:n + step, :], values, (((1,), (0,)), ((), ())),
                                       preferred_element_type=jnp.float32)
             scale = weight[n:n + step, :]
@@ -129,12 +128,18 @@
             total = total + jnp.sum(term.reshape(step // 8, 8, points), axis=0)
         line = jnp.sum(total, axis=0, keepdims=True)
         for c in range(cols):
-            dens[c, pl.ds(b, 1), :] = line[:, c * share:(c + 1) * share]
+            part = line[:, c * share:(c + 1) * share]
+            dens[c, pl.ds(b, 1), :] = part if h == 0 else dens[c, pl.ds(b, 1), :] + part
         local = jnp.sum(angular[b] * line, axis=1, keepdims=True)
         moment[...] += local * jnp.where(atoms == atom[b], 1.0, 0.0)
         return carry
 
-    lax.fori_loop(0, batches, square, 0)
+    for h in range(HALVES):
+        for copy in sends[h]:
+            copy.wait()
+        for j in range(h * width // 128, (h + 1) * width // 128):
+            across[j * 128:(j + 1) * 128, :] = window[:, j * 128:(j + 1) * 128].T
+        lax.fori_loop(0, batches, functools.partial(square, h), 0)
 
     def exchange(axis, place, size, src_of, dst_of, sent, received):
         copies = []
@@ -206,7 +211,7 @@
             vmem((cols, lm, 128), single),
             vmem((rows, lm, 128), single),
             vmem((lm, 128), single),
-            dma, dma((DEPTH,)), dma, dma((rows - 1,)), dma((rows - 1,)),
+            dma, dma((DEPTH,)), dma, dma((HALVES, rows - 1)), dma((HALVES, rows - 1)),
             dma((cols - 1,)), dma((cols - 1,)), dma((cols - 1,)), dma((cols - 1,)),
             dma((rows - 1,)), dma((rows - 1,)),
         ],

time: 94.2 us -> 105 us (1.11)
  Pallas kernels: 83.9 us -> 94.7 us
    pallas_call x1, Pallas kernels: 83.9 us -> 94.7 us  [fused(): pl.pallas_call(functools.partial(kernel, rows, cols, owned), out_shape=(j...]
where the time goes in v3:
time: 105 us
  Pallas kernels  94.7 us (90%)
  local copies, waits for them, and re-layouts  9.35 us (9%)
    pallas_call x1, Pallas kernels, fused(): pl.pallas_call(functools.partial(kernel, rows, cols, owned), out_shape=(j...  94.7 us
    unnamed x2, local copies, waits for them, and re-layouts  7.9 us

profile of v3, /device:TPU:0, one launch (start us, length us, event | category | flops | bytes accessed | tf_op | source)
XLA Modules:
  0.0 104.7 jit_solution(10409771106249150982)
XLA Ops:
  0.6 6.6 %copy.9.harmonics = f32[40,49,512]{2,1,0:T(8,128)} copy(f32[40,49,512]{2,0,1:T(8,128)} %param.13) | data formatting | bytes 8028160 | tf_op args[6]
  7.2 94.7 %shard_map.86 = (f32[40,128]{1,0:T(8,128)}, f32[64,49]{1,0:T(8,128)}) custom-call(bf16[768,1024]{1,0:T(8,128)(2,1)} %coeffs.1, f32[8,128]{1,0:T(8,128)} %bitcast.1, bf16[40,512,512]{2,1,0:T(8,128)(2,1)} %basis.1, s32[40,512]{1,0:T(8,128)} %index.1, s32[40]{0:T(128)} %count.1, s32[40]{0:T(128)} %atom.1, f32[40,49,512]{2,1,0:T(8,128)} %copy.9.harmonics), custom_call_target="tpu_custom_call" | custom-call | tf_op jit(solution)/shard_map/pallas_call | solution.py:196
  101.9 1.5 %copy.10 = f32[64,49]{0,1:T(8,128)} copy(f32[64,49]{1,0:T(8,128)} %get-tuple-element.3) | data formatting | bytes 25088 | tf_op jit(solution)/shard_map/pallas_call | solution.py:196
  103.3 1.3 %copy.12 = f32[40,128]{1,0:T(8,128)} copy(f32[40,128]{1,0:T(8,128)} %get-tuple-element.6) | data formatting | bytes 40960
